TPU v7x, 32 devices: a whole 2x2x4 slice. The times are simulated.
32 devices in a mesh: rows: 4 (over y, x), feat: 8 (over z, core).
Axes of the slice: x: 2, y: 2, z: 4, core: 2. Of those that a mesh axis runs over, the one named last changes fastest.
Arguments:
- bins: int32 [256, 32768], P(None, ('rows', 'feat')), may hold values from 0 to 255
- leaf: int32 [32768], P(('rows', 'feat')), may hold values from 0 to 1
- grad: bfloat16 [32, 32768], P(None, ('rows', 'feat')), may hold values from -15.55 to 15.55
- hess: bfloat16 [32, 32768], P(None, ('rows', 'feat')), may hold values from 0.049804688 to 1
Outputs:
- gains: float32 [256, 2, 256], P(('rows', 'feat'))
- best: float32 [2], replicated
All inputs are finite; a program needn't handle non-finite values.
Results may differ from a plain program's by a relative error of at most 0.0003.
Values may be sent and summed in bfloat16 or wider, within the bound.
A program may use at most 128 MiB of HBM per device.

v0:
```python
import math
import jax
import jax.numpy as jnp
from jax import lax
from jax.sharding import PartitionSpec as P

F = 256
B = 256
LEAVES = 2


def leaf_weighted(both, leaf_row, leaves):
    nodes = jnp.arange(leaves, dtype=jnp.float32)[:, None]
    hot = (leaf_row.astype(jnp.float32) == nodes).astype(jnp.bfloat16)
    return (hot[:, None, :] * both[None, :, :]).reshape(leaves * both.shape[0], both.shape[1])


def bin_counts(codes, weighted, bin_total):
    levels = jnp.arange(bin_total, dtype=jnp.int32)
    onehot = (codes[:, :, None] == levels).astype(jnp.bfloat16)
    return jnp.einsum("frb,cr->fbc", onehot, weighted, preferred_element_type=jnp.float32)


def split_gains(hist, totals, outputs):
    count = hist.shape[0]
    cum = jnp.cumsum(hist, axis=1).reshape(count, B, LEAVES, 2, outputs)
    tot = totals.reshape(LEAVES, 2, outputs)
    left_grad = cum[:, :, :, 0, :]
    left_hess = cum[:, :, :, 1, :]
    all_grad = tot[:, 0, :]
    all_hess = tot[:, 1, :]
    right_grad = all_grad - left_grad
    right_hess = all_hess - left_hess
    score = (
        left_grad * left_grad / (left_hess + 1.0)
        + right_grad * right_grad / (right_hess + 1.0)
        - all_grad * all_grad / (all_hess + 1.0)
    )
    gains = 0.5 / outputs * jnp.sum(score, axis=-1)
    return jnp.transpose(gains, (0, 2, 1))


def shards(bins, leaf, grad, hess):
    outputs = grad.shape[0]
    shard = bins.shape[1]
    devices = lax.axis_size("rows") * lax.axis_size("feat")
    owned = F // devices
    both = jnp.concatenate([grad, hess], axis=0)
    leaf_row = leaf[None, :]
    weighted = leaf_weighted(both, leaf_row, LEAVES)
    columns = weighted.shape[0]
    codes_mine = lax.all_to_all(bins, ("rows", "feat"), split_axis=0, concat_axis=1, tiled=True)
    initial = jnp.zeros((owned, B, columns), jnp.float32)
    both_piece = lax.all_gather(both, ("rows", "feat"), axis=1, tiled=True)
    leaf_piece = lax.all_gather(leaf_row.astype(jnp.bfloat16), ("rows", "feat"), axis=1, tiled=True)
    length = both_piece.shape[1]
    width = math.gcd(length, 8 * shard)

    def step(index, total):
        offset = index * width
        part_codes = lax.dynamic_slice_in_dim(codes_mine, offset, width, 1)
        part_both = lax.dynamic_slice_in_dim(both_piece, offset, width, 1)
        part_leaf = lax.dynamic_slice_in_dim(leaf_piece, offset, width, 1)
        return total + bin_counts(part_codes, leaf_weighted(part_both, part_leaf, LEAVES), B)

    hist = lax.fori_loop(0, length // width, step, initial)
    totals = lax.psum(jnp.sum(weighted, axis=1, dtype=jnp.float32), ("rows", "feat"))
    gains = split_gains(hist, totals, outputs)
    best = lax.pmax(jnp.max(gains, axis=(0, 2)), ("rows", "feat"))
    return (gains, best)


def solution(mesh):
    return jax.shard_map(
        shards,
        mesh=mesh,
        in_specs=(
            P(None, ("rows", "feat")),
            P(("rows", "feat")),
            P(None, ("rows", "feat")),
            P(None, ("rows", "feat")),
        ),
        out_specs=(P(("rows", "feat"), None, None), P()),
        check_vma=False,
    )
```

profile of v0, /device:TPU:0, one launch (start us, length us, event | category | flops | bytes accessed | tf_op | source)
XLA Modules:
  0.0 226.1 jit_solution(3870619815995787336)
XLA Ops:
  7.2 0.0 copy-start.2
  7.2 0.0 all-gather.3.cloned.1.call-start
  7.2 0.8 constant_dynamic-update-slice_fusion.1
  8.1 0.8 constant_dynamic-update-slice_fusion
  8.9 0.0 copy-start
  8.9 0.6 copy-done
  9.5 0.0 all-gather.3.cloned.1.call-update
  9.6 0.0 copy-start.1
  9.6 7.3 %all-to-all-start = ((s32[32,8,1024]{2,1,0:T(8,128)}), s32[32,8,1024]{2,1,0:T(8,128)S(1)}, u32[]{:S(2)}, u32[]{:S(2)}) async-start(s32[32,8,1024]{2,1,0:T(8,128)} %bitcast.44), calls=%async_computation | async-start | bytes 2097152 | tf_op jit(solution)/shard_map/all_to_all | solution.py:52
  16.9 0.0 copy-done.2
  17.0 0.0 copy-done.1
  17.0 0.1 convert_reduce_fusion
  17.1 0.1 reshape.98
  17.2 60.4 %all-gather = bf16[32768]{0:T(1024)(128)(2,1)S(1)} all-gather(bf16[1024]{0:T(1024)(128)(2,1)S(1)} %get-tuple-element.128), channel_id=2, replica_groups=mesh['rows'=4,'feat'=8] {'rows','feat'}, dimensions={0}, use_global_device_ids=true | all-gather | bytes 67584 | tf_op jit(solution)/shard_map/all_gather | solution.py:55
  77.6 0.1 reshape.101
  77.6 37.5 %psum.7 = f32[2,2,32]{2,1,0:T(2,128)S(1)} all-reduce(f32[2,2,32]{2,1,0:T(2,128)S(1)} %reshape.98), channel_id=1, replica_groups=mesh['rows'=4,'feat'=8] {'rows','feat'}, use_global_device_ids=true, to_apply=%region_5.6 | all-reduce | flops 128 | bytes 1024 | tf_op jit(solution)/shard_map/psum | solution.py:67
  115.2 0.0 all-to-all-done
  115.2 0.0 all-gather.3.cloned.1.call-done
  115.2 58.8 %while.14 = (s32[]{:T(128)}, f32[8,256,128]{2,1,0:T(8,128)}, s32[8,32768]{1,0:T(8,128)S(1)}, bf16[1,32768]{1,0:T(2,128)(2,1)S(1)}, bf16[64,32768]{1,0:T(8,128)(2...) while((s32[]{:T(128)}, f32[8,256,128]{2,1,0:T(8,128)}, s32[8,32768]{1,0:T(8,128)S(1)}, ...), condition=%wide.region_1.0_spmd.clone, body=%wide.region_0.0_spmd.clone.sunk | while | flops 4313358336 | bytes 10371233 | solution.py:66
  115.2 1.3 constant_dynamic-slice_fusion.4
  116.6 0.2 broadcast_multiply_fusion.2
  116.8 12.3 %fusion.12 = f32[8,256,128]{2,1,0:T(8,128)} fusion(bf16[128,8192,1]{1,0,2:T(8,128)(2,1)S(1)} %bitcast.39, s32[8,8192]{1,0:T(8,128)S(1)} %constant_dynamic-slice_fusion.5, f32[8,256,128]{2,1,0:T(8,128)} %get-tuple-element.172, pred[]{:T(512)S(6)} %compare.3), kind=kOutput, calls=%fused_computation.3.clone.1 | convolution fusion | flops 4312268800 | bytes 4456449 | tf_op jit(solution)/shard_map/while/body/eval_jaxpr/frb,cr->fbc/dot_general | solution.py:21
  129.2 1.3 constant_dynamic-slice_fusion.4
  130.6 0.2 broadcast_multiply_fusion.2
  130.8 13.3 %fusion.12 = f32[8,256,128]{2,1,0:T(8,128)} fusion(bf16[128,8192,1]{1,0,2:T(8,128)(2,1)S(1)} %bitcast.39, s32[8,8192]{1,0:T(8,128)S(1)} %constant_dynamic-slice_fusion.5, f32[8,256,128]{2,1,0:T(8,128)} %get-tuple-element.172, pred[]{:T(512)S(6)} %compare.3), kind=kOutput, calls=%fused_computation.3.clone.1 | convolution fusion | flops 4312268800 | bytes 4456449 | tf_op jit(solution)/shard_map/while/body/eval_jaxpr/frb,cr->fbc/dot_general | solution.py:21
  144.1 1.3 constant_dynamic-slice_fusion.4
  145.5 0.2 broadcast_multiply_fusion.2
  145.7 13.4 %fusion.12 = f32[8,256,128]{2,1,0:T(8,128)} fusion(bf16[128,8192,1]{1,0,2:T(8,128)(2,1)S(1)} %bitcast.39, s32[8,8192]{1,0:T(8,128)S(1)} %constant_dynamic-slice_fusion.5, f32[8,256,128]{2,1,0:T(8,128)} %get-tuple-element.172, pred[]{:T(512)S(6)} %compare.3), kind=kOutput, calls=%fused_computation.3.clone.1 | convolution fusion | flops 4312268800 | bytes 4456449 | tf_op jit(solution)/shard_map/while/body/eval_jaxpr/frb,cr->fbc/dot_general | solution.py:21
  159.1 1.3 constant_dynamic-slice_fusion.4
  160.4 0.2 broadcast_multiply_fusion.2
  160.6 13.4 %fusion.12 = f32[8,256,128]{2,1,0:T(8,128)} fusion(bf16[128,8192,1]{1,0,2:T(8,128)(2,1)S(1)} %bitcast.39, s32[8,8192]{1,0:T(8,128)S(1)} %constant_dynamic-slice_fusion.5, f32[8,256,128]{2,1,0:T(8,128)} %get-tuple-element.172, pred[]{:T(512)S(6)} %compare.3), kind=kOutput, calls=%fused_computation.3.clone.1 | convolution fusion | flops 4312268800 | bytes 4456449 | tf_op jit(solution)/shard_map/while/body/eval_jaxpr/frb,cr->fbc/dot_general | solution.py:21
  174.0 1.8 fusion.3
  175.8 0.1 fusion.5
  175.9 0.1 broadcast_add_fusion
  176.0 0.4 copy.15
  176.4 0.4 subtract_reduce_fusion
  176.8 0.7 multiply_reduce_fusion
  177.5 41.8 %pmax.7 = f32[2]{0:T(128)} all-reduce(f32[2]{0:T(128)S(1)} %get-tuple-element.125), channel_id=1, replica_groups=mesh['rows'=4,'feat'=8] {'rows','feat'}, use_global_device_ids=true, to_apply=%region_8.9 | all-reduce | flops 2 | bytes 16 | tf_op jit(solution)/shard_map/pmax | solution.py:69
  (18 shorter events, 0.4 us)
Async XLA Ops:
  7.2 9.8 %copy-start.2 = (s32[1024]{0:T(1024)S(1)}, s32[1024]{0:T(1024)}, u32[]{:S(2)}) copy-start(s32[1024]{0:T(1024)} %param.7) | copy-start | bytes 12292
  7.2 108.0 %all-gather.3.cloned.1.call-start = ((), (), s32[]{:S(2)}) async-start(), calls=%async_computation.1 | async-start | bytes 4325376 | tf_op jit(solution)/shard_map/all_gather | solution.py:54
  8.9 0.6 copy-start
  9.6 7.4 %copy-start.1 = (bf16[64,1024]{1,0:T(8,128)(2,1)S(1)}, bf16[64,1024]{1,0:T(8,128)(2,1)}, u32[]{:S(2)}) copy-start(bf16[64,1024]{1,0:T(8,128)(2,1)} %copy-done) | copy-start | bytes 393220
  9.6 105.6 %all-to-all-start = ((s32[32,8,1024]{2,1,0:T(8,128)}), s32[32,8,1024]{2,1,0:T(8,128)S(1)}, u32[]{:S(2)}, u32[]{:S(2)}) async-start(s32[32,8,1024]{2,1,0:T(8,128)} %bitcast.44), calls=%async_computation | async-start | bytes 2097152 | tf_op jit(solution)/shard_map/all_to_all | solution.py:52
Sparse Core Ops, SparseCore 0:
  11.0 66.5 all-gather.2
where the time goes:
time: 227 us; the launch traced here: 226 us
  blocking collectives  140 us (62%)
  matrix products  52.4 us (23%)
  between operations  14.1 us (6%)
  local copies, waits for them, and re-layouts  8.17 us (4%)
  starting transfers between devices  7.37 us (3%)
  other arithmetic  4.15 us (2%)
    all_gather x1, blocking collectives, shards(): lax.all_gather(leaf_row.astype(jnp.bfloat16), ('rows', 'feat'), axis=1, t...  60.4 us
    dot_general x4, matrix products, bin_counts(): jnp.einsum('frb,cr->fbc', onehot, weighted, preferred_element_type=jnp.fl...  52.4 us
    pmax x1, blocking collectives, shards(): best = lax.pmax(jnp.max(gains, axis=(0, 2)), ('rows', 'feat'))  41.8 us
    psum x1, blocking collectives, shards(): lax.psum(jnp.sum(weighted, axis=1, dtype=jnp.float32), ('rows', 'feat'))  37.5 us
    all_to_all x1, starting transfers between devices, shards(): lax.all_to_all(bins, ('rows', 'feat'), split_axis=0, concat_axis=1, tiled...  7.33 us
    dynamic_slice x4, local copies, waits for them, and re-layouts, step(): part_both = lax.dynamic_slice_in_dim(both_piece, offset, width, 1)  5.17 us
  transfers between devices with their start and end apart: 2, of which 0 were waited for; matrix products, arithmetic and copies ran while one was open for 0% of the time, Pallas kernels for 0%

commit v1 on v0

--- a/solution.py
+++ b/solution.py
@@ -64,7 +64,9 @@
         return total + bin_counts(part_codes, leaf_weighted(part_both, part_leaf, LEAVES), B)
 
     hist = lax.fori_loop(0, length // width, step, initial)
-    totals = lax.psum(jnp.sum(weighted, axis=1, dtype=jnp.float32), ("rows", "feat"))
+    totals = jnp.sum(
+        lax.all_gather(jnp.sum(weighted, axis=1, dtype=jnp.float32), ("rows", "feat")), axis=0
+    )
     gains = split_gains(hist, totals, outputs)
     best = lax.pmax(jnp.max(gains, axis=(0, 2)), ("rows", "feat"))
     return (gains, best)

time: 227 us -> 223 us (0.982)
  blocking collectives: 140 us -> 136 us
    all_gather x0 -> x1, blocking collectives: none -> 59.8 us  [shards(): lax.all_gather(jnp.sum(weighted, axis=1, dtype=jnp.float32), ('rows', 'fe...]
    psum x1 -> x0, blocking collectives: 37.5 us -> none  [shards(): lax.psum(jnp.sum(weighted, axis=1, dtype=jnp.float32), ('rows', 'feat'))]
    all_gather x1, blocking collectives: 60.4 us -> 36.9 us  [shards(): lax.all_gather(leaf_row.astype(jnp.bfloat16), ('rows', 'feat'), axis=1, t...]
    pmax x1, blocking collectives: 41.8 us -> 39.3 us  [shards(): best = lax.pmax(jnp.max(gains, axis=(0, 2)), ('rows', 'feat'))]
where the time goes in v1:
time: 223 us
  blocking collectives  136 us (61%)
  matrix products  52.4 us (23%)
  between operations  14.2 us (6%)
  local copies, waits for them, and re-layouts  8.26 us (4%)
  starting transfers between devices  7.37 us (3%)
  other arithmetic  4.2 us (2%)
    all_gather x1, blocking collectives, shards(): lax.all_gather(jnp.sum(weighted, axis=1, dtype=jnp.float32), ('rows', 'fe...  59.8 us
    dot_general x4, matrix products, bin_counts(): jnp.einsum('frb,cr->fbc', onehot, weighted, preferred_element_type=jnp.fl...  52.4 us
    pmax x1, blocking collectives, shards(): best = lax.pmax(jnp.max(gains, axis=(0, 2)), ('rows', 'feat'))  39.3 us
    all_gather x1, blocking collectives, shards(): lax.all_gather(leaf_row.astype(jnp.bfloat16), ('rows', 'feat'), axis=1, t...  36.9 us
    all_to_all x1, starting transfers between devices, shards(): lax.all_to_all(bins, ('rows', 'feat'), split_axis=0, concat_axis=1, tiled...  7.33 us
    dynamic_slice x4, local copies, waits for them, and re-layouts, step(): part_both = lax.dynamic_slice_in_dim(both_piece, offset, width, 1)  5.17 us
  transfers between devices with their start and end apart: 2, of which 0 were waited for; matrix products, arithmetic and copies ran while one was open for 0% of the time, Pallas kernels for 0%

profile of v1, /device:TPU:0, one launch (start us, length us, event | category | flops | bytes accessed | tf_op | source)
XLA Modules:
  0.0 222.6 jit_solution(5283076173714647127)
XLA Ops:
  7.2 0.0 copy-start.2
  7.2 0.0 all-gather.4.cloned.1.call-start
  7.2 0.8 constant_dynamic-update-slice_fusion.1
  8.1 0.8 constant_dynamic-update-slice_fusion
  8.9 0.0 copy-start
  8.9 0.6 copy-done
  9.5 0.0 all-gather.4.cloned.1.call-update
  9.6 0.0 copy-start.1
  9.6 7.3 %all-to-all-start = ((s32[32,8,1024]{2,1,0:T(8,128)}), s32[32,8,1024]{2,1,0:T(8,128)S(1)}, u32[]{:S(2)}, u32[]{:S(2)}) async-start(s32[32,8,1024]{2,1,0:T(8,128)} %bitcast.44), calls=%async_computation | async-start | bytes 2097152 | tf_op jit(solution)/shard_map/all_to_all | solution.py:52
  16.9 0.0 copy-done.2
  17.0 0.0 copy-done.1
  17.0 0.1 convert_reduce_fusion
  17.1 0.1 reshape.102
  17.2 59.8 %all-gather.1 = f32[32,1,128]{2,1,0:T(1,128)S(1)} all-gather(f32[1,1,128]{2,1,0:T(1,128)S(1)} %reshape.102), channel_id=1, replica_groups=mesh['rows'=4,'feat'=8] {'rows','feat'}, dimensions={0}, use_global_device_ids=true | all-gather | bytes 16896 | tf_op jit(solution)/shard_map/all_gather | solution.py:68
  77.0 0.1 reduce_sum.28
  77.1 0.1 reshape.99
  77.2 36.9 %all-gather = bf16[32768]{0:T(1024)(128)(2,1)S(1)} all-gather(bf16[1024]{0:T(1024)(128)(2,1)S(1)} %get-tuple-element.128), channel_id=2, replica_groups=mesh['rows'=4,'feat'=8] {'rows','feat'}, dimensions={0}, use_global_device_ids=true | all-gather | bytes 67584 | tf_op jit(solution)/shard_map/all_gather | solution.py:55
  114.1 0.1 reshape.101
  114.2 0.0 all-to-all-done
  114.2 0.0 all-gather.4.cloned.1.call-done
  114.2 58.8 %while.14 = (s32[]{:T(128)}, f32[8,256,128]{2,1,0:T(8,128)}, s32[8,32768]{1,0:T(8,128)S(1)}, bf16[1,32768]{1,0:T(2,128)(2,1)S(1)}, bf16[64,32768]{1,0:T(8,128)(2...) while((s32[]{:T(128)}, f32[8,256,128]{2,1,0:T(8,128)}, s32[8,32768]{1,0:T(8,128)S(1)}, ...), condition=%wide.region_1.0_spmd.clone, body=%wide.region_0.0_spmd.clone.sunk | while | flops 4313358336 | bytes 10371233 | solution.py:66
  114.2 1.3 constant_dynamic-slice_fusion.4
  115.6 0.2 broadcast_multiply_fusion.2
  115.8 12.3 %fusion.12 = f32[8,256,128]{2,1,0:T(8,128)} fusion(bf16[128,8192,1]{1,0,2:T(8,128)(2,1)S(1)} %bitcast.39, s32[8,8192]{1,0:T(8,128)S(1)} %constant_dynamic-slice_fusion.5, f32[8,256,128]{2,1,0:T(8,128)} %get-tuple-element.172, pred[]{:T(512)S(6)} %compare.3), kind=kOutput, calls=%fused_computation.3.clone.1 | convolution fusion | flops 4312268800 | bytes 4456449 | tf_op jit(solution)/shard_map/while/body/eval_jaxpr/frb,cr->fbc/dot_general | solution.py:21
  128.1 1.3 constant_dynamic-slice_fusion.4
  129.5 0.2 broadcast_multiply_fusion.2
  129.7 13.4 %fusion.12 = f32[8,256,128]{2,1,0:T(8,128)} fusion(bf16[128,8192,1]{1,0,2:T(8,128)(2,1)S(1)} %bitcast.39, s32[8,8192]{1,0:T(8,128)S(1)} %constant_dynamic-slice_fusion.5, f32[8,256,128]{2,1,0:T(8,128)} %get-tuple-element.172, pred[]{:T(512)S(6)} %compare.3), kind=kOutput, calls=%fused_computation.3.clone.1 | convolution fusion | flops 4312268800 | bytes 4456449 | tf_op jit(solution)/shard_map/while/body/eval_jaxpr/frb,cr->fbc/dot_general | solution.py:21
  143.1 1.3 constant_dynamic-slice_fusion.4
  144.5 0.2 broadcast_multiply_fusion.2
  144.7 13.4 %fusion.12 = f32[8,256,128]{2,1,0:T(8,128)} fusion(bf16[128,8192,1]{1,0,2:T(8,128)(2,1)S(1)} %bitcast.39, s32[8,8192]{1,0:T(8,128)S(1)} %constant_dynamic-slice_fusion.5, f32[8,256,128]{2,1,0:T(8,128)} %get-tuple-element.172, pred[]{:T(512)S(6)} %compare.3), kind=kOutput, calls=%fused_computation.3.clone.1 | convolution fusion | flops 4312268800 | bytes 4456449 | tf_op jit(solution)/shard_map/while/body/eval_jaxpr/frb,cr->fbc/dot_general | solution.py:21
  158.0 1.3 constant_dynamic-slice_fusion.4
  159.4 0.2 broadcast_multiply_fusion.2
  159.6 13.3 %fusion.12 = f32[8,256,128]{2,1,0:T(8,128)} fusion(bf16[128,8192,1]{1,0,2:T(8,128)(2,1)S(1)} %bitcast.39, s32[8,8192]{1,0:T(8,128)S(1)} %constant_dynamic-slice_fusion.5, f32[8,256,128]{2,1,0:T(8,128)} %get-tuple-element.172, pred[]{:T(512)S(6)} %compare.3), kind=kOutput, calls=%fused_computation.3.clone.1 | convolution fusion | flops 4312268800 | bytes 4456449 | tf_op jit(solution)/shard_map/while/body/eval_jaxpr/frb,cr->fbc/dot_general | solution.py:21
  173.0 1.8 fusion.3
  174.8 0.1 fusion.5
  174.9 0.1 broadcast_add_fusion
  175.0 0.4 copy.15
  175.4 0.4 subtract_reduce_fusion
  175.7 0.7 multiply_reduce_fusion
  176.5 39.3 %pmax.7 = f32[2]{0:T(128)} all-reduce(f32[2]{0:T(128)S(1)} %get-tuple-element.125), channel_id=1, replica_groups=mesh['rows'=4,'feat'=8] {'rows','feat'}, use_global_device_ids=true, to_apply=%region_8.9 | all-reduce | flops 2 | bytes 16 | tf_op jit(solution)/shard_map/pmax | solution.py:71
  (18 shorter events, 0.4 us)
Async XLA Ops:
  7.2 9.8 %copy-start.2 = (s32[1024]{0:T(1024)S(1)}, s32[1024]{0:T(1024)}, u32[]{:S(2)}) copy-start(s32[1024]{0:T(1024)} %param.7) | copy-start | bytes 12292
  7.2 107.0 %all-gather.4.cloned.1.call-start = ((), (), s32[]{:S(2)}) async-start(), calls=%async_computation.1 | async-start | bytes 4325376 | tf_op jit(solution)/shard_map/all_gather | solution.py:54
  8.9 0.6 copy-start
  9.6 7.4 %copy-start.1 = (bf16[64,1024]{1,0:T(8,128)(2,1)S(1)}, bf16[64,1024]{1,0:T(8,128)(2,1)}, u32[]{:S(2)}) copy-start(bf16[64,1024]{1,0:T(8,128)(2,1)} %copy-done) | copy-start | bytes 393220
  9.6 104.6 %all-to-all-start = ((s32[32,8,1024]{2,1,0:T(8,128)}), s32[32,8,1024]{2,1,0:T(8,128)S(1)}, u32[]{:S(2)}, u32[]{:S(2)}) async-start(s32[32,8,1024]{2,1,0:T(8,128)} %bitcast.44), calls=%async_computation | async-start | bytes 2097152 | tf_op jit(solution)/shard_map/all_to_all | solution.py:52
Sparse Core Ops, SparseCore 0:
  11.0 66.4 all-gather.3
